TPU v7x, 512 devices: a 8x2x16 block of a 8x8x16 slice. The times are simulated.
512 devices in a mesh: groups: 2 (over y), seq: 16 (over z), fsdp: 8 (over x), sub: 2 (over core).
Axes of the slice: x: 8, y: 2, z: 16, core: 2. Of those that a mesh axis runs over, the one named last changes fastest.
The devices are a block of a 8x8x16 slice.
Arguments:
- tokens: bfloat16 [8192, 8192], P(('groups', 'seq')), parts along dimension 0, may hold values from -400 to 400
- norm_gain: float32 [8192], replicated, may hold values from 0.1 to 1.9
- w_query: bfloat16 [32, 16, 8192], P(('seq', 'sub'), 'fsdp'), may hold values from -0.0625 to 0.0625
- w_key: bfloat16 [32, 16, 8192], P(('seq', 'sub'), 'fsdp'), may hold values from -0.0625 to 0.0625
- w_value: bfloat16 [32, 128, 8192], P(('seq', 'sub'), 'fsdp'), may hold values from -5 to 5
- head_gain: float32 [128], replicated, may hold values from 0.1 to 1.9
- w_out: bfloat16 [32, 128, 8192], P('seq', None, ('fsdp', 'sub')), may hold values from -0.09375 to 0.09375
Outputs:
- mixed: bfloat16 [8192, 8192], P(('groups', 'seq'), ('fsdp', 'sub')), parts along dimension 0
There are 2 independent parts, one for each index of `groups`. A program takes and returns all parts, laid end to end along the dimension named above; an argument that names none is the same for every part. Nothing has to cross between parts.
All inputs are finite; a program needn't handle non-finite values.
Results may differ from a plain program's by a relative error of at most 0.0084.
Values may be sent and summed in bfloat16 or wider, within the bound.
A program may use at most 64 MiB of HBM per device.

v0:
```python
import math
import jax
import jax.numpy as jnp
import numpy as np
from jax import lax
from jax.sharding import PartitionSpec as P

BLOCK = 512


def laid_out(pieces, dim):
    pieces = jnp.moveaxis(pieces, 0, dim)
    dims = pieces.shape
    return pieces.reshape(*dims[:dim], dims[dim] * dims[dim + 1], *dims[dim + 2 :])


def copy_for_each(array, axis):
    copies = jnp.broadcast_to(array, (lax.axis_size(axis), *array.shape))
    return lax.all_to_all(copies, axis, split_axis=0, concat_axis=0, tiled=True)


def gathered_copies(array, axis, dim):
    return laid_out(copy_for_each(array, axis), dim)


def taylor_first(vectors):
    feature_count = vectors.shape[0]
    first_row, second_row = np.triu_indices(feature_count, 1)
    cross_terms = vectors[first_row] * vectors[second_row] / 4.0
    squares = vectors * vectors / (4.0 * math.sqrt(2.0))
    leading = jnp.ones((1,) + vectors.shape[1:], jnp.float32)
    return jnp.concatenate([leading, vectors / 2.0, cross_terms, squares], 0)


def head_norm(numerator, head_gain, channel_axis):
    widened = numerator.astype(jnp.float32)
    meansq = jnp.mean(widened * widened, axis=channel_axis, keepdims=True)
    gain_shape = tuple((-1 if axis_pos == channel_axis else 1 for axis_pos in range(widened.ndim)))
    return (widened * lax.rsqrt(meansq + 1e-06) * head_gain.reshape(gain_shape)).astype(
        jnp.bfloat16
    )


def attend(queries, key_vectors, values_local):
    length = queries.shape[1]
    nblocks = length // BLOCK
    channels = values_local.shape[0]
    query_feats = taylor_first(queries.astype(jnp.float32)).astype(jnp.bfloat16)
    key_feats = taylor_first(key_vectors.astype(jnp.float32)).astype(jnp.bfloat16)
    taylor_width = query_feats.shape[0]
    contrib = jnp.einsum(
        "fbj,ebj->bfe",
        key_feats.reshape(taylor_width, nblocks, BLOCK),
        values_local.reshape(channels, nblocks, BLOCK),
        preferred_element_type=jnp.float32,
    )
    prefix = jnp.concatenate([jnp.zeros_like(contrib[:1]), jnp.cumsum(contrib[:-1], axis=0)], 0)
    prior_state = prefix.astype(jnp.bfloat16)
    carried = jnp.einsum(
        "bfe,fbt->bet",
        prior_state,
        query_feats.reshape(taylor_width, nblocks, BLOCK),
        preferred_element_type=jnp.float32,
    )
    earlier = lax.broadcasted_iota(jnp.int32, (BLOCK, BLOCK), 0)
    column_pos = lax.broadcasted_iota(jnp.int32, (BLOCK, BLOCK), 1)
    causal = earlier <= column_pos

    def one_block(block_index):
        offset = block_index * BLOCK
        query_block = lax.dynamic_slice_in_dim(queries, offset, BLOCK, 1)
        key_block = lax.dynamic_slice_in_dim(key_vectors, offset, BLOCK, 1)
        value_block = lax.dynamic_slice_in_dim(values_local, offset, BLOCK, 1)
        scores = jnp.einsum("fj,ft->jt", key_block, query_block, preferred_element_type=jnp.float32)
        kernel = 1.0 + scores / 4.0 + scores * scores / 32.0
        weight = jnp.where(causal, kernel, 0.0).astype(jnp.bfloat16)
        return jnp.einsum("ej,jt->et", value_block, weight, preferred_element_type=jnp.float32)

    local_part = lax.map(one_block, jnp.arange(nblocks, dtype=jnp.int32))
    numerator = (local_part + carried).astype(jnp.bfloat16)
    return jnp.transpose(numerator, (1, 0, 2)).reshape(channels, length)


def per_device(tokens, norm_gain, w_query, w_key, w_value, head_gain, w_out):
    feat_dev = w_query.shape[1]
    inputs = tokens.astype(jnp.float32)
    meansq = jnp.mean(inputs * inputs, axis=1, keepdims=True)
    normed = (inputs * lax.rsqrt(meansq + 1e-05) * norm_gain).astype(jnp.bfloat16)
    stacked = jnp.concatenate([w_query, w_key, w_value], 1)
    head_weights = lax.all_gather(stacked, "seq", axis=0, tiled=True)
    projected = jnp.einsum(
        "hcd,td->hct", head_weights, normed, preferred_element_type=jnp.float32
    ).astype(jnp.bfloat16)
    by_head = lax.all_to_all(projected, "seq", split_axis=0, concat_axis=2, tiled=True)
    qk_local = by_head[:, : 2 * feat_dev]
    values_local = by_head[0, 2 * feat_dev :]
    qk_whole = gathered_copies(qk_local, "fsdp", 0)
    length = qk_whole.shape[2]
    queries = qk_whole[:, :feat_dev].reshape(-1, length)
    key_vectors = qk_whole[:, feat_dev:].reshape(-1, length)
    numerator = attend(queries, key_vectors, values_local)
    out_weights = lax.all_gather(w_out, "seq", axis=0, tiled=True)
    heads_total = out_weights.shape[0]
    head_width = out_weights.shape[1]
    by_token = lax.all_to_all(numerator[None], "seq", split_axis=2, concat_axis=0, tiled=True)
    everyone = gathered_copies(by_token[None], ("fsdp", "sub"), 0)
    arranged = everyone.reshape(
        lax.axis_size("fsdp"),
        lax.axis_size("sub"),
        everyone.shape[1],
        everyone.shape[2],
        everyone.shape[3],
    )
    arranged = jnp.transpose(arranged, (2, 1, 0, 3, 4)).reshape(heads_total, head_width, -1)
    attended = head_norm(arranged, head_gain, 1)
    mixed = jnp.einsum("het,hed->td", attended, out_weights, preferred_element_type=jnp.float32)
    return mixed.astype(jnp.bfloat16)


def solution(mesh):
    in_specs = (
        P(("groups", "seq"), None),
        P(),
        P(("seq", "sub"), "fsdp", None),
        P(("seq", "sub"), "fsdp", None),
        P(("seq", "sub"), "fsdp", None),
        P(),
        P("seq", None, ("fsdp", "sub")),
    )
    out_specs = P(("groups", "seq"), ("fsdp", "sub"))
    return jax.shard_map(
        per_device, mesh=mesh, in_specs=in_specs, out_specs=out_specs, check_vma=False
    )
```

profile of v0, /device:TPU:65, one launch (start us, length us, event | category | flops | bytes accessed | tf_op | source)
XLA Modules:
  0.0 342.6 jit_solution(4627285938782507637)
XLA Ops:
  6.6 1.9 pad_maximum_fusion
  8.5 3.1 fusion.18
  11.7 119.0 %all-gather.3.cloned.1.call-done = bf16[16,20,8192]{2,1,0:T(8,128)(2,1)} async-done(((bf16[1,20,8192]{2,1,0:T(8,128)(2,1)}), bf16[16,20,8192]{2,1,0:T(8,128)(2,1)}) %all-gather.3.cloned.1.call-update) | async-done | bytes 5242896 | tf_op jit(solution)/shard_map/all_gather | solution.py:90
  130.6 6.7 %fusion.45 = bf16[16,20,256]{2,1,0:T(8,128)(2,1)} fusion(bf16[16,20,8192]{2,1,0:T(8,128)(2,1)} %all-gather.3.cloned.1.call-done, bf16[256,8192]{1,0:T(8,128)(2,1)} %param.17, f32[8192]{0:T(1024)S(1)} %copy-done.6, f32[256]{0:T(256)S(1)} %add_rsqrt_fusion), kind=kOutput, calls=%fused_computation.54 | convolution fusion | flops 1350647808 | bytes 9634816 | tf_op jit(solution)/shard_map/hcd,td->hct/dot_general | solution.py:91
  137.3 9.1 %all-to-all-start = ((bf16[16,20,256]{2,1,0:T(8,128)(2,1)}), bf16[16,20,256]{2,1,0:T(8,128)(2,1)S(1)}, u32[]{:S(2)}, u32[]{:S(2)}) async-start(bf16[16,20,256]{2,1,0:T(8,128)(2,1)} %fusion.45), calls=%async_computation | async-start | bytes 393216 | tf_op jit(solution)/shard_map/all_to_all | solution.py:94
  147.3 11.2 %all-to-all-done = bf16[16,20,256]{2,1,0:T(8,128)(2,1)S(1)} async-done(((bf16[16,20,256]{2,1,0:T(8,128)(2,1)}), bf16[16,20,256]{2,1,0:T(8,128)(2,1)S(1)}, u32[]{:S(2)}, u32[]{:S(2)}) %all-to-all-start) | async-done | bytes 163872 | tf_op jit(solution)/shard_map/all_to_all | solution.py:94
  159.4 6.4 %all-to-all-start.1 = ((bf16[8,1,4,4096]{3,2,1,0:T(4,128)(2,1)}), bf16[8,1,4,4096]{3,2,1,0:T(4,128)(2,1)S(1)}, u32[]{:S(2)}, u32[]{:S(2)}) async-start(bf16[8,1,4,4096]{3,2,1,0:T(4,128)(2,1)} %broadcast_in_dim.37), calls=%async_computation.1 | async-start | bytes 524288 | tf_op jit(solution)/shard_map/all_to_all | solution.py:19
  167.3 7.9 %all-to-all-done.1 = bf16[8,1,4,4096]{3,2,1,0:T(4,128)(2,1)S(1)} async-done(((bf16[8,1,4,4096]{3,2,1,0:T(4,128)(2,1)}), bf16[8,1,4,4096]{3,2,1,0:T(4,128)(2,1)S(1)}, u32[]{:S(2)}, u32[]{:S(2)}) %all-to-all-start.1) | async-done | bytes 262176 | tf_op jit(solution)/shard_map/all_to_all | solution.py:19
  175.4 1.4 fusion.62
  176.9 2.5 gather_fusion
  179.3 2.5 gather_fusion.1
  181.9 1.3 gather_fusion.2
  183.2 2.5 gather_fusion.3
  185.7 2.4 multiply_convert_fusion.3
  191.5 1.8 multiply_convert_fusion.2
  195.3 19.3 %while.11 = (s32[]{:T(128)}, f32[8,16,512]{2,1,0:T(8,128)S(1)}, s32[8]{0:T(128)S(1)}, bf16[16,4096]{1,0:T(8,128)(2,1)}, bf16[16,4096]{1,0:T(8,128)(2,1)S(1)}, /*...) while((s32[]{:T(128)}, f32[8,16,512]{2,1,0:T(8,128)S(1)}, ...), condition=%wide.region_2.3_spmd.clone, body=%wide.region_1.0_spmd.clone.sunk | while | flops 18874372 | bytes 84127 | solution.py:79
  215.3 2.7 copy.76
  218.5 22.6 %reduce.4 = bf16[4096,16]{1,0:T(8,128)(2,1)S(1)} reduce(bf16[4096,1,16]{2,1,0:T(2,128)(2,1)S(1)} %bitcast.70, bf16[]{:T(256)} %broadcast.136), dimensions={1}, to_apply=%bitcast.56.reduce_sub_computation | reduce | bytes 262146
  242.3 22.1 %all_to_all.43 = bf16[16,2,2048]{2,1,0:T(2,128)(2,1)S(1)} all-to-all(bf16[16,2,2048]{2,1,0:T(2,128)(2,1)S(1)} %reshape.133), channel_id=1, replica_groups=mesh['groups'=2,'seq'=16,'fsdp'=8,'sub'=2] {'seq'}, dimensions={0} | all-to-all | bytes 262144 | tf_op jit(solution)/shard_map/all_to_all | solution.py:105
  264.4 1.8 reshape.134
  266.2 2.0 copy.77
  268.5 57.5 %all_to_all.44 = bf16[16,1,16,16,256]{4,3,2,1,0:T(8,128)(2,1)S(1)} all-to-all(bf16[16,1,16,16,256]{4,3,2,1,0:T(8,128)(2,1)S(1)} %broadcast_in_dim.43), channel_id=1, replica_groups=mesh['groups'=2,'seq'=16,'fsdp'=8,'sub'=2] {'fsdp','sub'}, dimensions={0} | all-to-all | bytes 4194304 | tf_op jit(solution)/shard_map/all_to_all | solution.py:19
  326.6 2.6 copy.80
  330.2 5.5 %fusion.44 = bf16[256,512]{1,0:T(8,128)(2,1)} fusion(bf16[32,128,512]{2,1,0:T(8,128)(2,1)} %all-gather.5.cloned.1.call-done, f32[32,128,256]{2,1,0:T(8,128)} %bitcast.72, f32[128]{0:T(128)S(1)} %copy-done.7, f32[32,256]{1,0:T(8,128)S(1)} %rsqrt.21), kind=kOutput, calls=%fused_computation.53 | convolution fusion | flops 1077018624 | bytes 8684032 | tf_op jit(solution)/shard_map/het,hed->td/dot_general | solution.py:116
  (83 shorter events, 27.1 us)
Async XLA Ops:
  6.5 124.1 %copy-start.6 = (f32[8192]{0:T(1024)S(1)}, f32[8192]{0:T(1024)}, u32[]{:S(2)}) copy-start(f32[8192]{0:T(1024)} %param.18) | copy-start | bytes 98308
  6.5 124.1 %all-gather.3.cloned.1.call-start = ((), (), s32[]{:S(2)}) async-start(), calls=%async_computation.4 | async-start | bytes 6684672 | tf_op jit(solution)/shard_map/all_gather | solution.py:90
  11.6 135.6 %copy-start.5 = (s32[120]{0:T(128)S(1)}, s32[120]{0:T(128)}, u32[]{:S(2)}) copy-start(s32[120]{0:T(128)} %constant.78) | copy-start | bytes 1444
  11.6 135.6 %copy-start.4 = (s32[120]{0:T(128)S(1)}, s32[120]{0:T(128)}, u32[]{:S(2)}) copy-start(s32[120]{0:T(128)} %constant.79) | copy-start | bytes 1444
  137.3 21.2 %all-to-all-start = ((bf16[16,20,256]{2,1,0:T(8,128)(2,1)}), bf16[16,20,256]{2,1,0:T(8,128)(2,1)S(1)}, u32[]{:S(2)}, u32[]{:S(2)}) async-start(bf16[16,20,256]{2,1,0:T(8,128)(2,1)} %fusion.45), calls=%async_computation | async-start | bytes 393216 | tf_op jit(solution)/shard_map/all_to_all | solution.py:94
  146.4 183.8 %all-gather.5.cloned.1.call-start = ((), (), s32[]{:S(2)}) async-start(), calls=%async_computation.5 | async-start | bytes 4456448 | tf_op jit(solution)/shard_map/all_gather | solution.py:102
  159.4 15.8 %all-to-all-start.1 = ((bf16[8,1,4,4096]{3,2,1,0:T(4,128)(2,1)}), bf16[8,1,4,4096]{3,2,1,0:T(4,128)(2,1)S(1)}, u32[]{:S(2)}, u32[]{:S(2)}) async-start(bf16[8,1,4,4096]{3,2,1,0:T(4,128)(2,1)} %broadcast_in_dim.37), calls=%async_computation.1 | async-start | bytes 524288 | tf_op jit(solution)/shard_map/all_to_all | solution.py:19
  191.5 1.9 copy-start
  193.3 0.9 copy-start.1
  193.3 1.0 copy-start.2
  193.3 1.0 copy-start.3
  194.3 0.9 copy-start.8
  329.2 1.0 copy-start.7
Sparse Core Ops, SparseCore 0:
  9.4 121.1 all-gather.2
  149.3 71.7 all-gather.4
where the time goes:
time: 344 us; the launch traced here: 343 us
  waiting for transfers between devices  139 us (40%)
  blocking collectives  79.6 us (23%)
  other arithmetic  34.7 us (10%)
  local copies, waits for them, and re-layouts  32.1 us (9%)
  matrix products  22.6 us (7%)
  starting transfers between devices  15.6 us (5%)
  between operations  13.8 us (4%)
  loops' own time  5.26 us (2%)
    all_gather x1, waiting for transfers between devices, per_device(): head_weights = lax.all_gather(stacked, 'seq', axis=0, tiled=True)  119 us
    all_to_all x1, blocking collectives, copy_for_each(): return lax.all_to_all(copies, axis, split_axis=0, concat_axis=0, tiled=True)  57.5 us
    unnamed x1, other arithmetic  22.6 us
    all_to_all x1, blocking collectives, per_device(): lax.all_to_all(numerator[None], 'seq', split_axis=2, concat_axis=0, tiled...  22.1 us
    all_to_all x1, waiting for transfers between devices, per_device(): lax.all_to_all(projected, 'seq', split_axis=0, concat_axis=2, tiled=True)  11.2 us
    dot_general x8, matrix products, one_block(): jnp.einsum('ej,jt->et', value_block, weight, preferred_element_type=jnp.f...  9.3 us
    all_to_all x1, starting transfers between devices, per_device(): lax.all_to_all(projected, 'seq', split_axis=0, concat_axis=2, tiled=True)  9.07 us
    gather x4, local copies, waits for them, and re-layouts, taylor_first(): cross_terms = vectors[first_row] * vectors[second_row] / 4.0  8.71 us
  transfers between devices with their start and end apart: 4, of which 3 were waited for; matrix products, arithmetic and copies ran while one was open for 22% of the time, Pallas kernels for 0%

commit v1 on v0

--- a/solution.py
+++ b/solution.py
@@ -87,7 +87,10 @@
     meansq = jnp.mean(inputs * inputs, axis=1, keepdims=True)
     normed = (inputs * lax.rsqrt(meansq + 1e-05) * norm_gain).astype(jnp.bfloat16)
     stacked = jnp.concatenate([w_query, w_key, w_value], 1)
-    head_weights = lax.all_gather(stacked, "seq", axis=0, tiled=True)
+    size = lax.axis_size("seq")
+    blocks = jnp.stack([stacked for _ in range(size)])
+    blocks = lax.all_to_all(blocks, "seq", split_axis=0, concat_axis=0)
+    head_weights = jnp.concatenate(blocks, axis=0)
     projected = jnp.einsum(
         "hcd,td->hct", head_weights, normed, preferred_element_type=jnp.float32
     ).astype(jnp.bfloat16)

time: 344 us -> 543 us (1.58)
  waiting for transfers between devices: 139 us -> 289 us
  starting transfers between devices: 15.6 us -> 62.8 us
    all_to_all x0 -> x1, waiting for transfers between devices: none -> 268 us  [per_device(): blocks = lax.all_to_all(blocks, 'seq', split_axis=0, concat_axis=0)]
    all_gather x1 -> x0, waiting for transfers between devices: 119 us -> none  [per_device(): head_weights = lax.all_gather(stacked, 'seq', axis=0, tiled=True)]
    all_to_all x0 -> x1, starting transfers between devices: none -> 44.2 us  [per_device(): blocks = lax.all_to_all(blocks, 'seq', split_axis=0, concat_axis=0)]
  transfers between devices with their start and end apart: 4 -> 4, of which waited for: 3 -> 3; matrix products, arithmetic and copies ran while one was open for 22% -> 14% of each run, Pallas kernels for 0% -> 0%
where the time goes in v1:
time: 543 us; the launch traced here: 542 us
  waiting for transfers between devices  289 us (53%)
  blocking collectives  79.4 us (15%)
  starting transfers between devices  62.8 us (12%)
  local copies, waits for them, and re-layouts  35.5 us (7%)
  other arithmetic  34 us (6%)
  matrix products  22.6 us (4%)
  between operations  13.8 us (3%)
    all_to_all x1, waiting for transfers between devices, per_device(): blocks = lax.all_to_all(blocks, 'seq', split_axis=0, concat_axis=0)  268 us
    all_to_all x1, blocking collectives, copy_for_each(): return lax.all_to_all(copies, axis, split_axis=0, concat_axis=0, tiled=True)  57.5 us
    all_to_all x1, starting transfers between devices, per_device(): blocks = lax.all_to_all(blocks, 'seq', split_axis=0, concat_axis=0)  44.2 us
    unnamed x1, other arithmetic  22.6 us
    all_to_all x1, blocking collectives, per_device(): lax.all_to_all(numerator[None], 'seq', split_axis=2, concat_axis=0, tiled...  21.8 us
    all_to_all x1, waiting for transfers between devices, per_device(): lax.all_to_all(projected, 'seq', split_axis=0, concat_axis=2, tiled=True)  11.4 us
    all_to_all x1, starting transfers between devices, per_device(): lax.all_to_all(projected, 'seq', split_axis=0, concat_axis=2, tiled=True)  11.3 us
  transfers between devices with their start and end apart: 4, of which 3 were waited for; matrix products, arithmetic and copies ran while one was open for 14% of the time, Pallas kernels for 0%

profile of v1, /device:TPU:65, one launch (start us, length us, event | category | flops | bytes accessed | tf_op | source)
XLA Modules:
  0.0 541.8 jit_solution(9713140328975303488)
XLA Ops:
  7.7 3.4 stack.2
  11.1 44.2 %all-to-all-start = ((bf16[16,1,20,8192]{3,2,1,0:T(8,128)(2,1)}), bf16[16,1,20,8192]{3,2,1,0:T(8,128)(2,1)}, u32[]{:S(2)}, u32[]{:S(2)}) async-start(bf16[16,1,20,8192]{3,2,1,0:T(8,128)(2,1)} %stack.2), calls=%async_computation | async-start | bytes 12582912 | tf_op jit(solution)/shard_map/all_to_all | solution.py:92
  55.3 3.1 fusion.18
  58.5 268.4 %all-to-all-done = bf16[16,1,20,8192]{3,2,1,0:T(8,128)(2,1)} async-done(((bf16[16,1,20,8192]{3,2,1,0:T(8,128)(2,1)}), bf16[16,1,20,8192]{3,2,1,0:T(8,128)(2,1)}, u32[]{:S(2)}, u32[]{:S(2)}) %all-to-all-start) | async-done | bytes 5242912 | tf_op jit(solution)/shard_map/all_to_all | solution.py:92
  326.9 6.7 %fusion.46 = bf16[16,20,256]{2,1,0:T(8,128)(2,1)} fusion(bf16[256,8192]{1,0:T(8,128)(2,1)} %param.17, f32[8192]{0:T(1024)S(1)} %copy-done.6, f32[256]{0:T(256)S(1)} %add_rsqrt_fusion, bf16[16,1,20,8192]{3,2,1,0:T(8,128)(2,1)} %all-to-all-done), kind=kOutput, calls=%fused_computation.55 | convolution fusion | flops 1350647808 | bytes 9634816 | tf_op jit(solution)/shard_map/hcd,td->hct/dot_general | solution.py:94
  333.6 11.3 %all-to-all-start.1 = ((bf16[16,20,256]{2,1,0:T(8,128)(2,1)}), bf16[16,20,256]{2,1,0:T(8,128)(2,1)S(1)}, u32[]{:S(2)}, u32[]{:S(2)}) async-start(bf16[16,20,256]{2,1,0:T(8,128)(2,1)} %fusion.46), calls=%async_computation.1 | async-start | bytes 393216 | tf_op jit(solution)/shard_map/all_to_all | solution.py:97
  345.8 11.4 %all-to-all-done.1 = bf16[16,20,256]{2,1,0:T(8,128)(2,1)S(1)} async-done(((bf16[16,20,256]{2,1,0:T(8,128)(2,1)}), bf16[16,20,256]{2,1,0:T(8,128)(2,1)S(1)}, u32[]{:S(2)}, u32[]{:S(2)}) %all-to-all-start.1) | async-done | bytes 163872 | tf_op jit(solution)/shard_map/all_to_all | solution.py:97
  358.1 7.2 %all-to-all-start.2 = ((bf16[8,1,4,4096]{3,2,1,0:T(4,128)(2,1)}), bf16[8,1,4,4096]{3,2,1,0:T(4,128)(2,1)S(1)}, u32[]{:S(2)}, u32[]{:S(2)}) async-start(bf16[8,1,4,4096]{3,2,1,0:T(4,128)(2,1)} %broadcast_in_dim.37), calls=%async_computation.2 | async-start | bytes 524288 | tf_op jit(solution)/shard_map/all_to_all | solution.py:19
  366.7 8.0 %all-to-all-done.2 = bf16[8,1,4,4096]{3,2,1,0:T(4,128)(2,1)S(1)} async-done(((bf16[8,1,4,4096]{3,2,1,0:T(4,128)(2,1)}), bf16[8,1,4,4096]{3,2,1,0:T(4,128)(2,1)S(1)}, u32[]{:S(2)}, u32[]{:S(2)}) %all-to-all-start.2) | async-done | bytes 262176 | tf_op jit(solution)/shard_map/all_to_all | solution.py:19
  374.9 1.3 fusion.65
  376.3 2.5 gather_fusion
  378.8 2.5 gather_fusion.1
  382.7 2.5 gather_fusion.3
  385.1 2.4 multiply_convert_fusion.3
  391.0 1.8 multiply_convert_fusion.2
  394.8 19.3 %while.11 = (s32[]{:T(128)}, f32[8,16,512]{2,1,0:T(8,128)S(1)}, s32[8]{0:T(128)S(1)}, bf16[16,4096]{1,0:T(8,128)(2,1)}, bf16[16,4096]{1,0:T(8,128)(2,1)S(1)}, /*...) while((s32[]{:T(128)}, f32[8,16,512]{2,1,0:T(8,128)S(1)}, ...), condition=%wide.region_2.3_spmd.clone, body=%wide.region_1.0_spmd.clone.sunk | while | flops 18874372 | bytes 84127 | solution.py:79
  414.8 2.7 copy.76
  418.0 22.6 %reduce.4 = bf16[4096,16]{1,0:T(8,128)(2,1)S(1)} reduce(bf16[4096,1,16]{2,1,0:T(2,128)(2,1)S(1)} %bitcast.76, bf16[]{:T(256)} %broadcast.139), dimensions={1}, to_apply=%bitcast.63.reduce_sub_computation | reduce | bytes 262146
  441.8 21.8 %all_to_all.48 = bf16[16,2,2048]{2,1,0:T(2,128)(2,1)S(1)} all-to-all(bf16[16,2,2048]{2,1,0:T(2,128)(2,1)S(1)} %reshape.140), channel_id=1, replica_groups=mesh['groups'=2,'seq'=16,'fsdp'=8,'sub'=2] {'seq'}, dimensions={0} | all-to-all | bytes 262144 | tf_op jit(solution)/shard_map/all_to_all | solution.py:108
  463.6 1.8 reshape.141
  465.4 2.0 copy.77
  467.7 57.5 %all_to_all.49 = bf16[16,1,16,16,256]{4,3,2,1,0:T(8,128)(2,1)S(1)} all-to-all(bf16[16,1,16,16,256]{4,3,2,1,0:T(8,128)(2,1)S(1)} %broadcast_in_dim.43), channel_id=1, replica_groups=mesh['groups'=2,'seq'=16,'fsdp'=8,'sub'=2] {'fsdp','sub'}, dimensions={0} | all-to-all | bytes 4194304 | tf_op jit(solution)/shard_map/all_to_all | solution.py:19
  525.8 2.6 copy.80
  529.5 5.5 %fusion.45 = bf16[256,512]{1,0:T(8,128)(2,1)} fusion(bf16[32,128,512]{2,1,0:T(8,128)(2,1)} %all-gather.2.cloned.1.call-done, f32[32,128,256]{2,1,0:T(8,128)} %bitcast.78, f32[128]{0:T(128)S(1)} %copy-done.7, f32[32,256]{1,0:T(8,128)S(1)} %rsqrt.21), kind=kOutput, calls=%fused_computation.54 | convolution fusion | flops 1077018624 | bytes 8684032 | tf_op jit(solution)/shard_map/het,hed->td/dot_general | solution.py:119
  (83 shorter events, 29.4 us)
Async XLA Ops:
  11.1 315.8 %all-to-all-start = ((bf16[16,1,20,8192]{3,2,1,0:T(8,128)(2,1)}), bf16[16,1,20,8192]{3,2,1,0:T(8,128)(2,1)}, u32[]{:S(2)}, u32[]{:S(2)}) async-start(bf16[16,1,20,8192]{3,2,1,0:T(8,128)(2,1)} %stack.2), calls=%async_computation | async-start | bytes 12582912 | tf_op jit(solution)/shard_map/all_to_all | solution.py:92
  55.3 271.6 %copy-start.6 = (f32[8192]{0:T(1024)S(1)}, f32[8192]{0:T(1024)}, u32[]{:S(2)}) copy-start(f32[8192]{0:T(1024)} %param.18) | copy-start | bytes 98308
  58.4 287.3 %copy-start.5 = (s32[120]{0:T(128)S(1)}, s32[120]{0:T(128)}, u32[]{:S(2)}) copy-start(s32[120]{0:T(128)} %constant.78) | copy-start | bytes 1444
  58.5 287.3 %copy-start.4 = (s32[120]{0:T(128)S(1)}, s32[120]{0:T(128)}, u32[]{:S(2)}) copy-start(s32[120]{0:T(128)} %constant.79) | copy-start | bytes 1444
  333.6 23.6 %all-to-all-start.1 = ((bf16[16,20,256]{2,1,0:T(8,128)(2,1)}), bf16[16,20,256]{2,1,0:T(8,128)(2,1)S(1)}, u32[]{:S(2)}, u32[]{:S(2)}) async-start(bf16[16,20,256]{2,1,0:T(8,128)(2,1)} %fusion.46), calls=%async_computation.1 | async-start | bytes 393216 | tf_op jit(solution)/shard_map/all_to_all | solution.py:97
  344.9 184.6 %all-gather.2.cloned.1.call-start = ((), (), s32[]{:S(2)}) async-start(), calls=%async_computation.5 | async-start | bytes 4456448 | tf_op jit(solution)/shard_map/all_gather | solution.py:105
  358.1 16.5 %all-to-all-start.2 = ((bf16[8,1,4,4096]{3,2,1,0:T(4,128)(2,1)}), bf16[8,1,4,4096]{3,2,1,0:T(4,128)(2,1)S(1)}, u32[]{:S(2)}, u32[]{:S(2)}) async-start(bf16[8,1,4,4096]{3,2,1,0:T(4,128)(2,1)} %broadcast_in_dim.37), calls=%async_computation.2 | async-start | bytes 524288 | tf_op jit(solution)/shard_map/all_to_all | solution.py:19
  391.0 1.9 copy-start
  392.8 0.9 copy-start.1
  392.8 1.0 copy-start.2
  392.8 1.0 copy-start.3
  393.8 1.0 copy-start.8
  528.4 1.0 copy-start.7
Sparse Core Ops, SparseCore 0:
  347.8 73.5 all-gather.1
